TPU v7x, 32 devices: a whole 2x2x4 slice. The times are simulated.
32 devices in a mesh: gx: 2 (over y), gz: 4 (over z), gy: 4 (over x, core).
Axes of the slice: x: 2, y: 2, z: 4, core: 2. Of those that a mesh axis runs over, the one named last changes fastest.
Arguments:
- logits: float32 [256, 131072], P('gy', ('gx', 'gz')), may hold values from -60 to 250
Outputs:
- token_potential: float32 [131072], P(('gx', 'gz'))
- expert_potential: float32 [256], P('gy')
All inputs are finite; a program needn't handle non-finite values.
Results may differ from a plain program's by a relative error of at most 0.0001.
Values sent between devices are 32-bit elements; how exact they have to be, the bound alone decides.
A program may use at most 64 MiB of HBM per device.

v0:
```python
import jax
import jax.numpy as jnp
from jax import lax
from jax.sharding import PartitionSpec as P

ITERS = 3


def merged(array, axis, combine):
    everything = jax.tree.map(lambda part: lax.all_gather(part, axis), array)
    first = jax.tree.map(lambda part: part[0], everything)

    def turn(k, so_far):
        return combine(so_far, jax.tree.map(lambda part: part[k], everything))

    return lax.fori_loop(1, lax.axis_size(axis), turn, first)


def pair_join(first, second):
    top = jnp.maximum(first[0], second[0])
    return (top, first[1] * jnp.exp(first[0] - top) + second[1] * jnp.exp(second[0] - top))


def per_device(logits):
    local_experts = logits.shape[0]
    local_tokens = logits.shape[1]
    all_tokens = local_tokens * lax.axis_size("gx") * lax.axis_size("gz")
    all_experts = local_experts * lax.axis_size("gy")
    log_cap = jnp.log(jnp.float32(all_tokens) / jnp.float32(all_experts))
    token_potential = jnp.zeros((local_tokens,), jnp.float32)
    expert_potential = jnp.zeros((local_experts,), jnp.float32)
    for step in range(ITERS):
        shifted = logits + token_potential[None, :]
        top = jnp.max(shifted, axis=1)
        local_total = jnp.sum(jnp.exp(shifted - top[:, None]), axis=1)
        top, total = merged((top, local_total), ("gx", "gz"), pair_join)
        expert_potential = log_cap - (top + jnp.log(total))
        raised = logits + expert_potential[:, None]
        peak = jnp.max(raised, axis=0)
        local_summed = jnp.sum(jnp.exp(raised - peak[None, :]), axis=0)
        peak, summed = merged((peak, local_summed), "gy", pair_join)
        token_potential = -(peak + jnp.log(summed))
    return (token_potential, expert_potential)


def solution(mesh):
    in_specs = (P("gy", ("gx", "gz")),)
    out_specs = (P(("gx", "gz")), P("gy"))
    return jax.shard_map(
        per_device, mesh=mesh, in_specs=in_specs, out_specs=out_specs, check_vma=False
    )
```

profile of v0, /device:TPU:0, one launch (start us, length us, event | category | flops | bytes accessed | tf_op | source)
XLA Modules:
  0.0 130.6 jit_solution(10890844377879361667)
XLA Ops:
  0.6 2.5 %reduce_max.54 = f32[64]{0:T(128)S(1)} reduce(f32[64,16384]{1,0:T(8,128)} %param.13, f32[]{:T(128)} %constant.217.clone.1), dimensions={1}, to_apply=%region_0.0 | reduce | flops 1048512 | bytes 4194564 | tf_op jit(solution)/shard_map/reduce_max | solution.py:34
  3.1 0.6 dynamic-slice
  4.4 0.2 dynamic-update-slice
  4.6 2.9 %exponential_reduce_fusion.5 = f32[64]{0:T(128)S(1)} fusion(f32[64,16384]{1,0:T(8,128)} %param.13, f32[64]{0:T(128)S(1)} %reduce_max.54), kind=kLoop, calls=%fused_computation.32 | loop fusion | flops 2097088 | bytes 4194816 | tf_op jit(solution)/shard_map/reduce_sum | solution.py:35
  7.5 0.2 dynamic-update-slice.1
  7.8 23.3 %all-reduce.8 = (f32[512]{0:T(512)S(1)}, f32[512]{0:T(512)S(1)}) all-reduce(f32[512]{0:T(512)S(1)} %dynamic-update-slice, f32[512]{0:T(512)S(1)} %dynamic-update-slice.1), channel_id=2, replica_groups=mesh['gx'=2,'gz'=4,'gy'=4] {'gx','gz'}, use_global_device_ids=true, to_apply=%add | all-reduce | flops 1024 | bytes 8192
  31.1 0.1 reshape.15
  31.1 0.1 reshape.16
  31.2 0.3 while.102
  31.5 2.8 %add_reduce_fusion.4 = f32[16384]{0:T(1024)S(1)} fusion(f32[64,16384]{1,0:T(8,128)} %param.13, f32[64]{0:T(128)S(1)} %add_subtract_fusion.2), kind=kLoop, calls=%fused_computation.37 | loop fusion | flops 2080768 | bytes 4260096 | tf_op jit(solution)/shard_map/reduce_max | solution.py:39
  34.3 5.8 %all-gather.2 = f32[65536]{0:T(1024)S(1)} all-gather(f32[16384]{0:T(1024)S(1)} %add_reduce_fusion.4), channel_id=4, replica_groups=mesh['gx'=2,'gz'=4,'gy'=4] {'gy'}, dimensions={0}, use_global_device_ids=true | all-gather | bytes 327680 | tf_op jit(solution)/shard_map/all_gather | solution.py:10
  40.1 0.9 exponential_reduce_fusion.4
  41.0 5.9 %all-gather.3 = f32[65536]{0:T(1024)S(1)} all-gather(f32[16384]{0:T(1024)S(1)} %exponential_reduce_fusion.4), channel_id=5, replica_groups=mesh['gx'=2,'gz'=4,'gy'=4] {'gy'}, dimensions={0}, use_global_device_ids=true | all-gather | bytes 327680 | tf_op jit(solution)/shard_map/all_gather | solution.py:10
  46.9 0.1 reshape.17
  47.0 0.1 reshape.18
  47.1 0.7 while.103
  47.1 0.1 constant_dynamic-slice_fusion.12
  47.2 0.1 multiply_add_fusion.6
  47.3 0.1 constant_dynamic-slice_fusion.12
  47.5 0.1 multiply_add_fusion.6
  47.6 0.1 constant_dynamic-slice_fusion.12
  47.7 0.1 multiply_add_fusion.6
  47.8 2.6 %add_reduce_fusion.3 = f32[64]{0:T(128)S(1)} fusion(f32[64,16384]{1,0:T(8,128)} %param.13, f32[16384]{0:T(1024)S(1)} %add_negate_fusion.2), kind=kLoop, calls=%fused_computation.36 | loop fusion | flops 2097088 | bytes 4260096 | tf_op jit(solution)/shard_map/reduce_max | solution.py:34
  50.4 0.2 dynamic-update-slice.2
  50.6 3.0 %exponential_reduce_fusion.3 = f32[64]{0:T(128)S(1)} fusion(f32[64,16384]{1,0:T(8,128)} %param.13, f32[64]{0:T(128)S(1)} %add_reduce_fusion.3, f32[16384]{0:T(1024)S(1)} %add_negate_fusion.2), kind=kLoop, calls=%fused_computation.30 | loop fusion | flops 3145664 | bytes 4260352 | tf_op jit(solution)/shard_map/reduce_sum | solution.py:35
  53.7 0.2 dynamic-update-slice.3
  53.9 17.2 %all-reduce.7 = (f32[512]{0:T(512)S(1)}, f32[512]{0:T(512)S(1)}) all-reduce(f32[512]{0:T(512)S(1)} %dynamic-update-slice.2, f32[512]{0:T(512)S(1)} %dynamic-update-slice.3), channel_id=6, replica_groups=mesh['gx'=2,'gz'=4,'gy'=4] {'gx','gz'}, use_global_device_ids=true, to_apply=%add.2 | all-reduce | flops 1024 | bytes 8192
  71.1 0.1 reshape.19
  71.2 0.1 reshape.20
  71.3 0.3 while.104
  71.6 2.8 %add_reduce_fusion.2 = f32[16384]{0:T(1024)S(1)} fusion(f32[64,16384]{1,0:T(8,128)} %param.13, f32[64]{0:T(128)S(1)} %add_subtract_fusion.1), kind=kLoop, calls=%fused_computation.35 | loop fusion | flops 2080768 | bytes 4260096 | tf_op jit(solution)/shard_map/reduce_max | solution.py:39
  74.4 5.8 %all-gather.6 = f32[65536]{0:T(1024)S(1)} all-gather(f32[16384]{0:T(1024)S(1)} %add_reduce_fusion.2), channel_id=8, replica_groups=mesh['gx'=2,'gz'=4,'gy'=4] {'gy'}, dimensions={0}, use_global_device_ids=true | all-gather | bytes 327680 | tf_op jit(solution)/shard_map/all_gather | solution.py:10
  80.2 0.9 exponential_reduce_fusion.2
  81.0 5.9 %all-gather.7 = f32[65536]{0:T(1024)S(1)} all-gather(f32[16384]{0:T(1024)S(1)} %exponential_reduce_fusion.2), channel_id=9, replica_groups=mesh['gx'=2,'gz'=4,'gy'=4] {'gy'}, dimensions={0}, use_global_device_ids=true | all-gather | bytes 327680 | tf_op jit(solution)/shard_map/all_gather | solution.py:10
  86.9 0.1 reshape.21
  87.0 0.1 reshape.22
  87.1 0.7 while.105
  87.1 0.1 constant_dynamic-slice_fusion.13
  87.3 0.1 multiply_add_fusion.7
  87.4 0.1 constant_dynamic-slice_fusion.13
  87.5 0.1 multiply_add_fusion.7
  87.6 0.1 constant_dynamic-slice_fusion.13
  87.8 0.1 multiply_add_fusion.7
  87.9 2.6 %add_reduce_fusion.1 = f32[64]{0:T(128)S(1)} fusion(f32[64,16384]{1,0:T(8,128)} %param.13, f32[16384]{0:T(1024)S(1)} %add_negate_fusion.1), kind=kLoop, calls=%fused_computation.34 | loop fusion | flops 2097088 | bytes 4260096 | tf_op jit(solution)/shard_map/reduce_max | solution.py:34
  90.4 0.2 dynamic-update-slice.4
  90.7 3.0 %exponential_reduce_fusion.1 = f32[64]{0:T(128)S(1)} fusion(f32[64,16384]{1,0:T(8,128)} %param.13, f32[64]{0:T(128)S(1)} %add_reduce_fusion.1, f32[16384]{0:T(1024)S(1)} %add_negate_fusion.1), kind=kLoop, calls=%fused_computation.28 | loop fusion | flops 3145664 | bytes 4260352 | tf_op jit(solution)/shard_map/reduce_sum | solution.py:35
  93.7 0.2 dynamic-update-slice.5
  94.0 19.2 %all-reduce.6 = (f32[512]{0:T(512)S(1)}, f32[512]{0:T(512)S(1)}) all-reduce(f32[512]{0:T(512)S(1)} %dynamic-update-slice.4, f32[512]{0:T(512)S(1)} %dynamic-update-slice.5), channel_id=10, replica_groups=mesh['gx'=2,'gz'=4,'gy'=4] {'gx','gz'}, use_global_device_ids=true, to_apply=%add.4 | all-reduce | flops 1024 | bytes 8192
  113.2 0.1 reshape.23
  113.2 0.1 reshape.24
  113.3 0.3 while.106
  113.7 2.8 %add_reduce_fusion = f32[16384]{0:T(1024)S(1)} fusion(f32[64,16384]{1,0:T(8,128)} %param.13, f32[64]{0:T(128)S(1)} %add_subtract_fusion), kind=kLoop, calls=%fused_computation.33 | loop fusion | flops 2080768 | bytes 4260096 | tf_op jit(solution)/shard_map/reduce_max | solution.py:39
  116.4 5.8 %all-gather.10 = f32[65536]{0:T(1024)S(1)} all-gather(f32[16384]{0:T(1024)S(1)} %add_reduce_fusion), channel_id=12, replica_groups=mesh['gx'=2,'gz'=4,'gy'=4] {'gy'}, dimensions={0}, use_global_device_ids=true | all-gather | bytes 327680 | tf_op jit(solution)/shard_map/all_gather | solution.py:10
  122.2 0.9 exponential_reduce_fusion
  123.1 5.9 %all-gather.11 = f32[65536]{0:T(1024)S(1)} all-gather(f32[16384]{0:T(1024)S(1)} %exponential_reduce_fusion), channel_id=13, replica_groups=mesh['gx'=2,'gz'=4,'gy'=4] {'gy'}, dimensions={0}, use_global_device_ids=true | all-gather | bytes 327680 | tf_op jit(solution)/shard_map/all_gather | solution.py:10
  129.0 0.1 reshape.25
  129.1 0.1 reshape.26
  129.2 0.7 while.107
  129.2 0.1 constant_dynamic-slice_fusion.14
  129.5 0.1 constant_dynamic-slice_fusion.14
  129.6 0.1 multiply_add_fusion.8
  129.7 0.1 constant_dynamic-slice_fusion.14
  129.8 0.1 multiply_add_fusion.8
  129.9 0.6 add_negate_fusion
  (55 shorter events, 0.8 us)
Async XLA Ops:
  0.6 2.5 %copy-start.4 = (u32[32]{0:T(128)S(1)}, u32[32]{0:T(128)}, u32[]{:S(2)}) copy-start(u32[32]{0:T(128)} %constant.221) | copy-start | bytes 388
  31.5 8.6 %copy-start = (f32[64,16384]{1,0:T(8,128)S(1)}, f32[64,16384]{1,0:T(8,128)}, u32[]{:S(2)}) copy-start(f32[64,16384]{1,0:T(8,128)} %param.13) | copy-start | bytes 12582916
  71.6 8.6 %copy-start.1 = (f32[64,16384]{1,0:T(8,128)S(1)}, f32[64,16384]{1,0:T(8,128)}, u32[]{:S(2)}) copy-start(f32[64,16384]{1,0:T(8,128)} %param.13) | copy-start | bytes 12582916
  113.6 8.6 %copy-start.2 = (f32[64,16384]{1,0:T(8,128)S(1)}, f32[64,16384]{1,0:T(8,128)}, u32[]{:S(2)}) copy-start(f32[64,16384]{1,0:T(8,128)} %param.13) | copy-start | bytes 12582916
  113.6 9.5 %copy-start.3 = (f32[64]{0:T(128)}, f32[64]{0:T(128)S(1)}, u32[]{:S(2)}) copy-start(f32[64]{0:T(128)S(1)} %add_subtract_fusion) | copy-start | bytes 772
where the time goes:
time: 131 us
  blocking collectives  94.6 us (72%)
  other arithmetic  29.4 us (22%)
  local copies, waits for them, and re-layouts  4.46 us (3%)
  between operations  1.54 us (1%)
    unnamed x3, blocking collectives  59.7 us
    all_gather x6, blocking collectives, merged(): everything = jax.tree.map(lambda part: lax.all_gather(part, axis), array)  34.9 us
    reduce_sum x3, other arithmetic, per_device(): local_total = jnp.sum(jnp.exp(shifted - top[:, None]), axis=1)  8.93 us
    reduce_max x3, other arithmetic, per_device(): peak = jnp.max(raised, axis=0)  8.39 us
    reduce_max x3, other arithmetic, per_device(): top = jnp.max(shifted, axis=1)  7.6 us

commit v1 on v0

v1 whole, which is shorter than its diff:
```python
import functools

import jax
import jax.numpy as jnp
from jax import lax
from jax.experimental import pallas as pl
from jax.experimental.pallas import tpu as pltpu
from jax.sharding import PartitionSpec as P

ITERS = 3
LANES = 128
SUB = 8
MESH = pl.DeviceIdType.MESH


def kernel(nx, nz, ny, chunks, x_hbm, tok_ref, exp_ref, x, tops, sums, rows_out, rows_in,
           mine, theirs, peak, weight, scaled, first_tok, load_sem, es_sem, er_sem, ts_sem, tr_sem):
    experts, tokens = x.shape
    groups = experts // SUB
    blocks = tokens // LANES
    n = nx * nz
    stages = ny.bit_length() - 1
    per = blocks // chunks
    gx, gz, gy = lax.axis_index("gx"), lax.axis_index("gz"), lax.axis_index("gy")
    me = gx * nz + gz
    cap = float(tokens * n) / float(experts * ny)
    log_cap = jnp.log(jnp.full((1, LANES), cap, jnp.float32))

    loads = []
    for i in range(groups):
        rows = pl.ds(i * SUB, SUB)
        load = pltpu.make_async_copy(x_hbm.at[rows, :], x.at[rows, :], load_sem.at[i])
        load.start()
        loads.append(load)

    def peer(k):
        other = lax.rem(me + k, n)
        return (other // nz, lax.rem(other, nz), gy)

    def partner(stage):
        bit = 1 << stage
        up = lax.rem(gy // bit, 2)
        return (gx, gz, gy + bit - 2 * bit * up)

    barrier = pltpu.get_barrier_semaphore()

    def greet(k, carry):
        pl.semaphore_signal(barrier, inc=1, device_id=peer(k), device_id_type=MESH)
        return carry

    lax.fori_loop(1, n, greet, 0, unroll=n <= 8)
    for stage in range(stages):
        pl.semaphore_signal(barrier, inc=1, device_id=partner(stage), device_id_type=MESH)

    diag = (lax.broadcasted_iota(jnp.int32, (experts, LANES), 0)
            == lax.broadcasted_iota(jnp.int32, (experts, LANES), 1))

    def to_row(column):
        return jnp.sum(jnp.where(diag, jnp.broadcast_to(column, (experts, LANES)), 0.0),
                       axis=0, keepdims=True)

    def to_column(row):
        column = jnp.sum(jnp.where(diag, jnp.broadcast_to(row, (experts, LANES)), 0.0),
                         axis=1, keepdims=True)
        return jnp.broadcast_to(column, (experts, LANES))

    def exchange_rows(it, row):
        rows_out[it] = row

        def send(k, carry):
            pltpu.make_async_remote_copy(
                src_ref=rows_out.at[it], dst_ref=rows_in.at[it, k - 1],
                send_sem=es_sem.at[it], recv_sem=er_sem.at[it],
                device_id=peer(k), device_id_type=MESH).start()
            return carry

        lax.fori_loop(1, n, send, 0, unroll=n <= 8)
        whole = rows_in.at[it]
        pltpu.make_async_copy(whole, whole, er_sem.at[it]).wait()
        return [row] + [rows_in[it, k] for k in range(n - 1)]

    wide = 8 * LANES

    def fold(array, combine):
        parts = [array[:, k * LANES:(k + 1) * LANES] for k in range(array.shape[1] // LANES)]
        while len(parts) > 1:
            parts = [combine(parts[k], parts[k + 1]) for k in range(0, len(parts), 2)]
        return parts[0]

    for i in range(groups):
        rows = pl.ds(i * SUB, SUB)
        loads[i].wait()

        def higher(j, m):
            return jnp.maximum(m, x[rows, pl.ds(pl.multiple_of(j * wide, wide), wide)])

        m = fold(lax.fori_loop(1, tokens // wide, higher, x[rows, pl.ds(0, wide)], unroll=5),
                 jnp.maximum)
        tiled = jnp.concatenate([m] * 8, axis=1)

        def more(j, s):
            return s + jnp.exp(x[rows, pl.ds(pl.multiple_of(j * wide, wide), wide)] - tiled)

        s = fold(lax.fori_loop(0, tokens // wide, more, jnp.zeros((SUB, wide), jnp.float32),
                               unroll=4), jnp.add)
        tops[rows, :] = m
        sums[rows, :] = s

    lane_top = tops[...]
    top = jnp.max(lane_top, axis=1, keepdims=True)
    total = jnp.sum(sums[...] * jnp.exp(lane_top - top), axis=1, keepdims=True)
    local = to_row(top + jnp.log(total))

    pl.semaphore_wait(barrier, n - 1 + stages)

    parts = exchange_rows(0, local)
    top = functools.reduce(jnp.maximum, parts)
    total = functools.reduce(jnp.add, [jnp.exp(part - top) for part in parts])
    first_exp = log_cap - (top + jnp.log(total))
    factor = to_column(first_exp)

    def chunk(c):
        return pl.ds(c * per, per)

    def tok_copy(it, stage, c):
        return pltpu.make_async_remote_copy(
            src_ref=mine.at[it, stage, chunk(c), :], dst_ref=theirs.at[it, stage, chunk(c), :],
            send_sem=ts_sem.at[it, stage, c], recv_sem=tr_sem.at[it, stage, c],
            device_id=partner(stage), device_id_type=MESH)

    for it in range(ITERS):
        last = it == ITERS - 1
        for c in range(chunks):
            def column_pass(jj, carry):
                for u in range(SUB):
                    j = jj * SUB + u
                    lanes = pl.ds(pl.multiple_of(j * LANES, LANES), LANES)
                    if it == 0:
                        v = x[:, lanes] + factor
                        p = jnp.max(v, axis=0, keepdims=True)
                        e = jnp.exp(v - p)
                        x[:, lanes] = e
                        peak[pl.ds(j, 1), :] = p
                    else:
                        e = x[:, lanes] * factor
                    scaled[pl.ds(j, 1), :] = jnp.sum(e, axis=0, keepdims=True)
                return carry

            lax.fori_loop(c * per // SUB, (c + 1) * per // SUB, column_pass, 0)
            if it == 0:
                mine[it, 0, chunk(c), :] = peak[chunk(c), :] + jnp.log(scaled[chunk(c), :])
            else:
                mine[it, 0, chunk(c), :] = weight[chunk(c), :] * scaled[chunk(c), :]
            tok_copy(it, 0, c).start()

        acc = jnp.zeros((experts, LANES), jnp.float32)
        for stage in range(stages):
            for c in range(chunks):
                tok_copy(it, stage, c).wait_recv()
                a, b = mine[it, stage, chunk(c), :], theirs[it, stage, chunk(c), :]
                if it == 0:
                    t = jnp.maximum(a, b)
                    joined = t + jnp.log(jnp.exp(a - t) + jnp.exp(b - t))
                else:
                    joined = a + b
                if stage < stages - 1:
                    mine[it, stage + 1, chunk(c), :] = joined
                    tok_copy(it, stage + 1, c).start()
                    continue
                if last:
                    tok_ref[chunk(c), :] = first_tok[chunk(c), :] - jnp.log(joined)
                    continue
                if it == 0:
                    first_tok[chunk(c), :] = -joined
                    w = jnp.exp(peak[chunk(c), :] - joined)
                    weight[chunk(c), :] = w
                    scaled[chunk(c), :] = w
                else:
                    scaled[chunk(c), :] = weight[chunk(c), :] / joined

                def row_pass(jj, acc):
                    for u in range(SUB):
                        j = jj * SUB + u
                        lanes = pl.ds(pl.multiple_of(j * LANES, LANES), LANES)
                        acc = acc + x[:, lanes] * scaled[pl.ds(j, 1), :]
                    return acc

                acc = lax.fori_loop(c * per // SUB, (c + 1) * per // SUB, row_pass, acc)
        if not last:
            parts = exchange_rows(it + 1, to_row(jnp.sum(acc, axis=1, keepdims=True)))
            total = functools.reduce(jnp.add, parts)
            factor = to_column(cap / total)
            if it == ITERS - 2:
                exp_ref[...] = first_exp + (log_cap - jnp.log(total))

    for it in range(ITERS):
        whole = rows_in.at[it]
        pltpu.make_async_copy(whole, whole, es_sem.at[it]).wait()
        for stage in range(stages):
            for c in range(chunks):
                tok_copy(it, stage, c).wait_send()


def solution(mesh):
    nx, nz, ny = mesh.shape["gx"], mesh.shape["gz"], mesh.shape["gy"]
    n = nx * nz
    stages = ny.bit_length() - 1
    chunks = 4

    def per_device(logits):
        experts, tokens = logits.shape
        blocks = tokens // LANES
        f32 = jnp.float32
        plane = pltpu.VMEM((blocks, LANES), f32)
        tok, exp = pl.pallas_call(
            functools.partial(kernel, nx, nz, ny, chunks),
            out_shape=(jax.ShapeDtypeStruct((blocks, LANES), f32),
                       jax.ShapeDtypeStruct((1, LANES), f32)),
            in_specs=[pl.BlockSpec(memory_space=pl.ANY)],
            out_specs=(pl.BlockSpec(memory_space=pltpu.VMEM),) * 2,
            scratch_shapes=[
                pltpu.VMEM((experts, tokens), f32),
                pltpu.VMEM((experts, LANES), f32),
                pltpu.VMEM((experts, LANES), f32),
                pltpu.VMEM((ITERS, 1, LANES), f32),
                pltpu.VMEM((ITERS, n - 1, 1, LANES), f32),
                pltpu.VMEM((ITERS, stages, blocks, LANES), f32),
                pltpu.VMEM((ITERS, stages, blocks, LANES), f32),
                plane, plane, plane, plane,
                pltpu.SemaphoreType.DMA((experts // SUB,)),
                pltpu.SemaphoreType.DMA((ITERS,)),
                pltpu.SemaphoreType.DMA((ITERS,)),
                pltpu.SemaphoreType.DMA((ITERS, stages, chunks)),
                pltpu.SemaphoreType.DMA((ITERS, stages, chunks)),
            ],
            compiler_params=pltpu.CompilerParams(
                collective_id=0, has_side_effects=True, vmem_limit_bytes=60 * 1024 * 1024),
        )(logits)
        return tok.reshape(tokens), exp[0, :experts]

    return jax.shard_map(
        per_device, mesh=mesh, in_specs=(P("gy", ("gx", "gz")),),
        out_specs=(P(("gx", "gz")), P("gy")), check_vma=False)
```

time: 131 us -> 40.6 us (0.31)
  blocking collectives: 94.6 us -> 0 us
  Pallas kernels: 0 us -> 37.2 us
  other arithmetic: 29.4 us -> 0 us
  local copies, waits for them, and re-layouts: 4.46 us -> 2.59 us
    unnamed x3 -> x0, blocking collectives: 59.7 us -> none
    pallas_call x0 -> x1, Pallas kernels: none -> 37.2 us  [per_device(): pl.pallas_call(functools.partial(kernel, nx, nz, ny, chunks), out_shape=(...]
    all_gather x6 -> x0, blocking collectives: 34.9 us -> none  [merged(): everything = jax.tree.map(lambda part: lax.all_gather(part, axis), array)]
    reduce_max x6 -> x0, other arithmetic: 16 us -> none  [the longest x3 8.39 us: per_device(): peak = jnp.max(raised, axis=0)]
    reduce_sum x6 -> x0, other arithmetic: 11.5 us -> none  [the longest x3 8.93 us: per_device(): local_total = jnp.sum(jnp.exp(shifted - top[:, None]), axis=1)]
where the time goes in v1:
time: 40.6 us; the launch traced here: 40.4 us
  Pallas kernels  37.2 us (92%)
  local copies, waits for them, and re-layouts  2.59 us (6%)
  between operations  0.64 us (2%)
    pallas_call x1, Pallas kernels, per_device(): pl.pallas_call(functools.partial(kernel, nx, nz, ny, chunks), out_shape=(...  37.2 us
    unnamed x1, local copies, waits for them, and re-layouts  1.47 us
    squeeze x1, local copies, waits for them, and re-layouts, per_device(): return (tok.reshape(tokens), exp[0, :experts])  1.12 us

profile of v1, /device:TPU:0, one launch (start us, length us, event | category | flops | bytes accessed | tf_op | source)
XLA Modules:
  0.0 40.4 jit_solution(1355073378400744873)
XLA Ops:
  0.6 37.2 %shard_map.30 = (f32[128,128]{1,0:T(8,128)}, f32[1,128]{1,0:T(1,128)}) custom-call(f32[64,16384]{1,0:T(8,128)} %x_hbm.1), custom_call_target="tpu_custom_call" | custom-call | tf_op jit(solution)/shard_map/pallas_call | solution.py:215
  37.8 1.1 %slice_bitcast_fusion = f32[64]{0:T(128)} fusion(f32[1,128]{1,0:T(1,128)} %get-tuple-element.5), kind=kLoop, calls=%fused_computation | loop fusion | bytes 512 | tf_op jit(solution)/shard_map/squeeze | solution.py:239
  38.9 1.5 %copy.4 = f32[16384]{0:T(1024)} copy(f32[16384]{0:T(1024)} %bitcast.3) | data formatting | bytes 131072

commit v2 on v1

--- a/solution.py
+++ b/solution.py
@@ -14,7 +14,7 @@
 
 
 def kernel(nx, nz, ny, chunks, x_hbm, tok_ref, exp_ref, x, tops, sums, rows_out, rows_in,
-           mine, theirs, peak, weight, scaled, first_tok, load_sem, es_sem, er_sem, ts_sem, tr_sem):
+           mine, theirs, held, level, weight, partial, scaled, first_tok, load_sem, es_sem, er_sem, ts_sem, tr_sem):
     experts, tokens = x.shape
     groups = experts // SUB
     blocks = tokens // LANES
@@ -81,11 +81,18 @@
 
     wide = 8 * LANES
 
+    def pairwise(parts, combine):
+        while len(parts) > 1:
+            parts = [combine(*parts[k:k + 2]) if k + 1 < len(parts) else parts[k]
+                     for k in range(0, len(parts), 2)]
+        return parts[0]
+
     def fold(array, combine):
-        parts = [array[:, k * LANES:(k + 1) * LANES] for k in range(array.shape[1] // LANES)]
-        while len(parts) > 1:
-            parts = [combine(parts[k], parts[k + 1]) for k in range(0, len(parts), 2)]
-        return parts[0]
+        return pairwise([array[:, k * LANES:(k + 1) * LANES]
+                         for k in range(array.shape[1] // LANES)], combine)
+
+    def tree(array, combine):
+        return pairwise([array[k * SUB:(k + 1) * SUB] for k in range(groups)], combine)
 
     for i in range(groups):
         rows = pl.ds(i * SUB, SUB)
@@ -134,23 +141,29 @@
             def column_pass(jj, carry):
                 for u in range(SUB):
                     j = jj * SUB + u
-                    lanes = pl.ds(pl.multiple_of(j * LANES, LANES), LANES)
                     if it == 0:
+                        lanes = pl.ds(pl.multiple_of(j * LANES, LANES), LANES)
                         v = x[:, lanes] + factor
-                        p = jnp.max(v, axis=0, keepdims=True)
-                        e = jnp.exp(v - p)
-                        x[:, lanes] = e
-                        peak[pl.ds(j, 1), :] = p
+                        p = tree(v, jnp.maximum)
+                        e = jnp.exp(v - jnp.concatenate([p] * groups, axis=0))
+                        held[j] = e
+                        level[j] = p
+                        partial[j] = tree(e, jnp.add)
                     else:
-                        e = x[:, lanes] * factor
-                    scaled[pl.ds(j, 1), :] = jnp.sum(e, axis=0, keepdims=True)
+                        partial[j] = tree(held[j] * factor, jnp.add) * weight[j]
                 return carry
 
             lax.fori_loop(c * per // SUB, (c + 1) * per // SUB, column_pass, 0)
-            if it == 0:
-                mine[it, 0, chunk(c), :] = peak[chunk(c), :] + jnp.log(scaled[chunk(c), :])
-            else:
-                mine[it, 0, chunk(c), :] = weight[chunk(c), :] * scaled[chunk(c), :]
+            for g in range(c * per // SUB, (c + 1) * per // SUB):
+                eight = pl.ds(g * SUB, SUB)
+                s = [partial[eight, k, :] for k in range(SUB)]
+                if it == 0:
+                    p = [level[eight, k, :] for k in range(SUB)]
+                    t = pairwise(p, jnp.maximum)
+                    s = pairwise([s[k] * jnp.exp(p[k] - t) for k in range(SUB)], jnp.add)
+                    mine[it, 0, eight, :] = t + jnp.log(s)
+                else:
+                    mine[it, 0, eight, :] = pairwise(s, jnp.add)
             tok_copy(it, 0, c).start()
 
         acc = jnp.zeros((experts, LANES), jnp.float32)
@@ -172,17 +185,20 @@
                     continue
                 if it == 0:
                     first_tok[chunk(c), :] = -joined
-                    w = jnp.exp(peak[chunk(c), :] - joined)
-                    weight[chunk(c), :] = w
-                    scaled[chunk(c), :] = w
+                    scaled[chunk(c), :] = joined
                 else:
-                    scaled[chunk(c), :] = weight[chunk(c), :] / joined
+                    scaled[chunk(c), :] = 1.0 / joined
 
                 def row_pass(jj, acc):
                     for u in range(SUB):
                         j = jj * SUB + u
-                        lanes = pl.ds(pl.multiple_of(j * LANES, LANES), LANES)
-                        acc = acc + x[:, lanes] * scaled[pl.ds(j, 1), :]
+                        w = jnp.broadcast_to(scaled[pl.ds(j, 1), :], (SUB, LANES))
+                        if it == 0:
+                            w = jnp.exp(level[j] - w)
+                            weight[j] = w
+                        else:
+                            w = weight[j] * w
+                        acc = acc + held[j] * jnp.concatenate([w] * groups, axis=0)
                     return acc
 
                 acc = lax.fori_loop(c * per // SUB, (c + 1) * per // SUB, row_pass, acc)
@@ -214,8 +230,7 @@
         plane = pltpu.VMEM((blocks, LANES), f32)
         tok, exp = pl.pallas_call(
             functools.partial(kernel, nx, nz, ny, chunks),
-            out_shape=(jax.ShapeDtypeStruct((blocks, LANES), f32),
-                       jax.ShapeDtypeStruct((1, LANES), f32)),
+            out_shape=(pltpu.VMEM((blocks, LANES), f32), pltpu.VMEM((1, LANES), f32)),
             in_specs=[pl.BlockSpec(memory_space=pl.ANY)],
             out_specs=(pl.BlockSpec(memory_space=pltpu.VMEM),) * 2,
             scratch_shapes=[
@@ -226,7 +241,11 @@
                 pltpu.VMEM((ITERS, n - 1, 1, LANES), f32),
                 pltpu.VMEM((ITERS, stages, blocks, LANES), f32),
                 pltpu.VMEM((ITERS, stages, blocks, LANES), f32),
-                plane, plane, plane, plane,
+                pltpu.VMEM((blocks, experts, LANES), f32),
+                pltpu.VMEM((blocks, SUB, LANES), f32),
+                pltpu.VMEM((blocks, SUB, LANES), f32),
+                pltpu.VMEM((blocks, SUB, LANES), f32),
+                plane, plane,
                 pltpu.SemaphoreType.DMA((experts // SUB,)),
                 pltpu.SemaphoreType.DMA((ITERS,)),
                 pltpu.SemaphoreType.DMA((ITERS,)),

time: 40.6 us -> 36.3 us (0.89)
  Pallas kernels: 37.2 us -> 34.3 us
  local copies, waits for them, and re-layouts: 2.59 us -> 1.15 us
    pallas_call x1, Pallas kernels: 37.2 us -> 34.3 us  [per_device(): pl.pallas_call(functools.partial(kernel, nx, nz, ny, chunks), out_shape=(...]
    unnamed x1, local copies, waits for them, and re-layouts: 1.47 us -> 0.63 us
    squeeze x1, local copies, waits for them, and re-layouts: 1.12 us -> 0.51 us  [per_device(): return (tok.reshape(tokens), exp[0, :experts])]
where the time goes in v2:
time: 36.3 us; the launch traced here: 36.1 us
  Pallas kernels  34.3 us (94%)
  local copies, waits for them, and re-layouts  1.15 us (3%)
  between operations  0.64 us (2%)
    pallas_call x1, Pallas kernels, per_device(): pl.pallas_call(functools.partial(kernel, nx, nz, ny, chunks), out_shape=(...  34.3 us

profile of v2, /device:TPU:0, one launch (start us, length us, event | category | flops | bytes accessed | tf_op | source)
XLA Modules:
  0.0 36.1 jit_solution(7439264800501795254)
XLA Ops:
  0.6 34.3 %shard_map.30 = (f32[128,128]{1,0:T(8,128)S(1)}, f32[1,128]{1,0:T(1,128)S(1)}) custom-call(f32[64,16384]{1,0:T(8,128)} %x_hbm.1), custom_call_target="tpu_custom_call" | custom-call | tf_op jit(solution)/shard_map/pallas_call | solution.py:231
  35.0 0.6 %copy.4 = f32[16384]{0:T(1024)} copy(f32[16384]{0:T(1024)S(1)} %bitcast.3) | data formatting | bytes 131072
  35.6 0.5 %slice_bitcast_fusion = f32[64]{0:T(128)} fusion(f32[1,128]{1,0:T(1,128)S(1)} %get-tuple-element.5), kind=kLoop, calls=%fused_computation | loop fusion | bytes 512 | tf_op jit(solution)/shard_map/squeeze | solution.py:258

commit v3 on v2

--- a/solution.py
+++ b/solution.py
@@ -13,17 +13,20 @@
 MESH = pl.DeviceIdType.MESH
 
 
-def kernel(nx, nz, ny, chunks, x_hbm, tok_ref, exp_ref, x, tops, sums, rows_out, rows_in,
-           mine, theirs, held, level, weight, partial, scaled, first_tok, load_sem, es_sem, er_sem, ts_sem, tr_sem):
+def kernel(nx, nz, ny, chunks, x_hbm, tok_ref, exp_ref, x, y, tops, sums, rows_out, rows_in,
+           mine, theirs, held, level, weight, partial, scaled, first_tok, factors, load_sem, move_sem, home_sem, es_sem, er_sem, ts_sem, tr_sem):
     experts, tokens = x.shape
     groups = experts // SUB
-    blocks = tokens // LANES
-    n = nx * nz
-    stages = ny.bit_length() - 1
+    half = tokens // 2
+    blocks = half // LANES
+    spots = nx * nz
+    n = 2 * spots
+    stages = ny.bit_length() - 2
     per = blocks // chunks
     gx, gz, gy = lax.axis_index("gx"), lax.axis_index("gz"), lax.axis_index("gy")
-    me = gx * nz + gz
-    cap = float(tokens * n) / float(experts * ny)
+    core = lax.rem(gy, 2)
+    me = (gx * nz + gz) * 2 + core
+    cap = float(tokens * spots) / float(experts * ny)
     log_cap = jnp.log(jnp.full((1, LANES), cap, jnp.float32))
 
     loads = []
@@ -35,12 +38,15 @@
 
     def peer(k):
         other = lax.rem(me + k, n)
-        return (other // nz, lax.rem(other, nz), gy)
+        spot = other // 2
+        return (spot // nz, lax.rem(spot, nz), gy - core + lax.rem(other, 2))
 
     def partner(stage):
-        bit = 1 << stage
+        bit = 2 << stage
         up = lax.rem(gy // bit, 2)
         return (gx, gz, gy + bit - 2 * bit * up)
+
+    sibling = (gx, gz, gy + 1 - 2 * core)
 
     barrier = pltpu.get_barrier_semaphore()
 
@@ -48,21 +54,24 @@
         pl.semaphore_signal(barrier, inc=1, device_id=peer(k), device_id_type=MESH)
         return carry
 
-    lax.fori_loop(1, n, greet, 0, unroll=n <= 8)
+    lax.fori_loop(1, n, greet, 0, unroll=n <= 16)
     for stage in range(stages):
         pl.semaphore_signal(barrier, inc=1, device_id=partner(stage), device_id_type=MESH)
 
-    diag = (lax.broadcasted_iota(jnp.int32, (experts, LANES), 0)
-            == lax.broadcasted_iota(jnp.int32, (experts, LANES), 1))
-
-    def to_row(column):
-        return jnp.sum(jnp.where(diag, jnp.broadcast_to(column, (experts, LANES)), 0.0),
+    both = 2 * experts
+    row_id = lax.broadcasted_iota(jnp.int32, (both, LANES), 0)
+    lane_id = lax.broadcasted_iota(jnp.int32, (both, LANES), 1)
+    diag = row_id == lane_id
+    local_diag = row_id[:experts] + core * experts == lane_id[:experts]
+
+    def to_row(column, where):
+        return jnp.sum(jnp.where(where, jnp.broadcast_to(column, where.shape), 0.0),
                        axis=0, keepdims=True)
 
     def to_column(row):
-        column = jnp.sum(jnp.where(diag, jnp.broadcast_to(row, (experts, LANES)), 0.0),
+        column = jnp.sum(jnp.where(diag, jnp.broadcast_to(row, (both, LANES)), 0.0),
                          axis=1, keepdims=True)
-        return jnp.broadcast_to(column, (experts, LANES))
+        return jnp.broadcast_to(column, (both, LANES))
 
     def exchange_rows(it, row):
         rows_out[it] = row
@@ -74,7 +83,7 @@
                 device_id=peer(k), device_id_type=MESH).start()
             return carry
 
-        lax.fori_loop(1, n, send, 0, unroll=n <= 8)
+        lax.fori_loop(1, n, send, 0, unroll=n <= 16)
         whole = rows_in.at[it]
         pltpu.make_async_copy(whole, whole, er_sem.at[it]).wait()
         return [row] + [rows_in[it, k] for k in range(n - 1)]
@@ -92,7 +101,7 @@
                          for k in range(array.shape[1] // LANES)], combine)
 
     def tree(array, combine):
-        return pairwise([array[k * SUB:(k + 1) * SUB] for k in range(groups)], combine)
+        return pairwise([array[k * SUB:(k + 1) * SUB] for k in range(array.shape[0] // SUB)], combine)
 
     for i in range(groups):
         rows = pl.ds(i * SUB, SUB)
@@ -116,18 +125,33 @@
     lane_top = tops[...]
     top = jnp.max(lane_top, axis=1, keepdims=True)
     total = jnp.sum(sums[...] * jnp.exp(lane_top - top), axis=1, keepdims=True)
-    local = to_row(top + jnp.log(total))
+    local = jnp.where(lane_id[:1] // experts == core, to_row(top + jnp.log(total), local_diag), -1e30)
 
     pl.semaphore_wait(barrier, n - 1 + stages)
 
+    away = pl.ds(pl.multiple_of((1 - core) * half, LANES), half)
+    move = pltpu.make_async_remote_copy(
+        src_ref=x.at[:, away], dst_ref=y, send_sem=move_sem.at[0], recv_sem=move_sem.at[1],
+        device_id=sibling, device_id_type=MESH)
+    move.start()
     parts = exchange_rows(0, local)
     top = functools.reduce(jnp.maximum, parts)
     total = functools.reduce(jnp.add, [jnp.exp(part - top) for part in parts])
     first_exp = log_cap - (top + jnp.log(total))
     factor = to_column(first_exp)
+    factors[0] = factor[:experts]
+    factors[1] = factor[experts:]
+    move.wait_recv()
 
     def chunk(c):
         return pl.ds(c * per, per)
+
+    def home_copy(c):
+        rows = pl.ds(pl.multiple_of(core * blocks + c * per, SUB), per)
+        return pltpu.make_async_remote_copy(
+            src_ref=tok_ref.at[rows, :], dst_ref=tok_ref.at[rows, :],
+            send_sem=home_sem.at[0, c], recv_sem=home_sem.at[1, c],
+            device_id=sibling, device_id_type=MESH)
 
     def tok_copy(it, stage, c):
         return pltpu.make_async_remote_copy(
@@ -142,15 +166,20 @@
                 for u in range(SUB):
                     j = jj * SUB + u
                     if it == 0:
-                        lanes = pl.ds(pl.multiple_of(j * LANES, LANES), LANES)
-                        v = x[:, lanes] + factor
-                        p = tree(v, jnp.maximum)
-                        e = jnp.exp(v - jnp.concatenate([p] * groups, axis=0))
-                        held[j] = e
+                        lanes = pl.ds(pl.multiple_of(core * half + j * LANES, LANES), LANES)
+                        own = x[:, lanes] + factors[core]
+                        other = (y[:, pl.ds(pl.multiple_of(j * LANES, LANES), LANES)]
+                                 + factors[1 - core])
+                        p = jnp.maximum(tree(own, jnp.maximum), tree(other, jnp.maximum))
+                        tall = jnp.concatenate([p] * groups, axis=0)
+                        own, other = jnp.exp(own - tall), jnp.exp(other - tall)
+                        held[j, core] = own
+                        held[j, 1 - core] = other
                         level[j] = p
-                        partial[j] = tree(e, jnp.add)
+                        partial[j] = tree(own, jnp.add) + tree(other, jnp.add)
                     else:
-                        partial[j] = tree(held[j] * factor, jnp.add) * weight[j]
+                        e = held[j].reshape(both, LANES) * factor
+                        partial[j] = tree(e, jnp.add) * weight[j]
                 return carry
 
             lax.fori_loop(c * per // SUB, (c + 1) * per // SUB, column_pass, 0)
@@ -166,7 +195,7 @@
                     mine[it, 0, eight, :] = pairwise(s, jnp.add)
             tok_copy(it, 0, c).start()
 
-        acc = jnp.zeros((experts, LANES), jnp.float32)
+        acc = jnp.zeros((both, LANES), jnp.float32)
         for stage in range(stages):
             for c in range(chunks):
                 tok_copy(it, stage, c).wait_recv()
@@ -181,7 +210,9 @@
                     tok_copy(it, stage + 1, c).start()
                     continue
                 if last:
-                    tok_ref[chunk(c), :] = first_tok[chunk(c), :] - jnp.log(joined)
+                    rows = pl.ds(pl.multiple_of(core * blocks + c * per, SUB), per)
+                    tok_ref[rows, :] = first_tok[chunk(c), :] - jnp.log(joined)
+                    home_copy(c).start()
                     continue
                 if it == 0:
                     first_tok[chunk(c), :] = -joined
@@ -198,17 +229,21 @@
                             weight[j] = w
                         else:
                             w = weight[j] * w
-                        acc = acc + held[j] * jnp.concatenate([w] * groups, axis=0)
+                        acc = acc + held[j].reshape(both, LANES) * jnp.concatenate([w] * (2 * groups), axis=0)
                     return acc
 
                 acc = lax.fori_loop(c * per // SUB, (c + 1) * per // SUB, row_pass, acc)
         if not last:
-            parts = exchange_rows(it + 1, to_row(jnp.sum(acc, axis=1, keepdims=True)))
+            parts = exchange_rows(it + 1, to_row(jnp.sum(acc, axis=1, keepdims=True), diag))
             total = functools.reduce(jnp.add, parts)
             factor = to_column(cap / total)
             if it == ITERS - 2:
-                exp_ref[...] = first_exp + (log_cap - jnp.log(total))
-
+                final = first_exp + (log_cap - jnp.log(total))
+                exp_ref[...] = jnp.where(core == 0, final[:, :experts], final[:, experts:both])
+
+    for c in range(chunks):
+        home_copy(c).wait()
+    move.wait_send()
     for it in range(ITERS):
         whole = rows_in.at[it]
         pltpu.make_async_copy(whole, whole, es_sem.at[it]).wait()
@@ -219,34 +254,38 @@
 
 def solution(mesh):
     nx, nz, ny = mesh.shape["gx"], mesh.shape["gz"], mesh.shape["gy"]
-    n = nx * nz
-    stages = ny.bit_length() - 1
-    chunks = 4
+    n = 2 * nx * nz
+    stages = ny.bit_length() - 2
+    chunks = 2
 
     def per_device(logits):
         experts, tokens = logits.shape
-        blocks = tokens // LANES
+        blocks = tokens // LANES // 2
         f32 = jnp.float32
         plane = pltpu.VMEM((blocks, LANES), f32)
         tok, exp = pl.pallas_call(
             functools.partial(kernel, nx, nz, ny, chunks),
-            out_shape=(pltpu.VMEM((blocks, LANES), f32), pltpu.VMEM((1, LANES), f32)),
+            out_shape=(pltpu.VMEM((2 * blocks, LANES), f32), pltpu.VMEM((1, experts), f32)),
             in_specs=[pl.BlockSpec(memory_space=pl.ANY)],
             out_specs=(pl.BlockSpec(memory_space=pltpu.VMEM),) * 2,
             scratch_shapes=[
                 pltpu.VMEM((experts, tokens), f32),
+                pltpu.VMEM((experts, tokens // 2), f32),
                 pltpu.VMEM((experts, LANES), f32),
                 pltpu.VMEM((experts, LANES), f32),
                 pltpu.VMEM((ITERS, 1, LANES), f32),
                 pltpu.VMEM((ITERS, n - 1, 1, LANES), f32),
                 pltpu.VMEM((ITERS, stages, blocks, LANES), f32),
                 pltpu.VMEM((ITERS, stages, blocks, LANES), f32),
-                pltpu.VMEM((blocks, experts, LANES), f32),
+                pltpu.VMEM((blocks, 2, experts, LANES), f32),
                 pltpu.VMEM((blocks, SUB, LANES), f32),
                 pltpu.VMEM((blocks, SUB, LANES), f32),
                 pltpu.VMEM((blocks, SUB, LANES), f32),
                 plane, plane,
+                pltpu.VMEM((2, experts, LANES), f32),
                 pltpu.SemaphoreType.DMA((experts // SUB,)),
+                pltpu.SemaphoreType.DMA((2,)),
+                pltpu.SemaphoreType.DMA((2, chunks)),
                 pltpu.SemaphoreType.DMA((ITERS,)),
                 pltpu.SemaphoreType.DMA((ITERS,)),
                 pltpu.SemaphoreType.DMA((ITERS, stages, chunks)),
@@ -255,7 +294,7 @@
             compiler_params=pltpu.CompilerParams(
                 collective_id=0, has_side_effects=True, vmem_limit_bytes=60 * 1024 * 1024),
         )(logits)
-        return tok.reshape(tokens), exp[0, :experts]
+        return tok.reshape(tokens), exp.reshape(experts)
 
     return jax.shard_map(
         per_device, mesh=mesh, in_specs=(P("gy", ("gx", "gz")),),

time: 36.3 us -> 33.2 us (0.915)
  Pallas kernels: 34.3 us -> 31.3 us
    pallas_call x1, Pallas kernels: 34.3 us -> 31.3 us  [per_device(): pl.pallas_call(functools.partial(kernel, nx, nz, ny, chunks), out_shape=(...]
    unnamed x1 -> x2, local copies, waits for them, and re-layouts: 0.63 us -> 1.15 us
    squeeze x1 -> x0, local copies, waits for them, and re-layouts: 0.51 us -> none  [per_device(): return (tok.reshape(tokens), exp[0, :experts])]
where the time goes in v3:
time: 33.2 us; the launch traced here: 33 us
  Pallas kernels  31.3 us (94%)
  local copies, waits for them, and re-layouts  1.15 us (3%)
  between operations  0.64 us (2%)
    pallas_call x1, Pallas kernels, per_device(): pl.pallas_call(functools.partial(kernel, nx, nz, ny, chunks), out_shape=(...  31.3 us
    unnamed x2, local copies, waits for them, and re-layouts  1.15 us

profile of v3, /device:TPU:0, one launch (start us, length us, event | category | flops | bytes accessed | tf_op | source)
XLA Modules:
  0.0 33.0 jit_solution(16345950674208735631)
XLA Ops:
  0.6 31.3 %shard_map.30 = (f32[128,128]{1,0:T(8,128)S(1)}, f32[1,64]{1,0:T(1,128)S(1)}) custom-call(f32[64,16384]{1,0:T(8,128)} %x_hbm.1), custom_call_target="tpu_custom_call" | custom-call | tf_op jit(solution)/shard_map/pallas_call | solution.py:266
  31.9 0.6 %copy.5 = f32[16384]{0:T(1024)} copy(f32[16384]{0:T(1024)S(1)} %bitcast.2) | data formatting | bytes 131072
  32.5 0.5 %copy.6 = f32[64]{0:T(128)} copy(f32[64]{0:T(128)S(1)} %bitcast.3) | data formatting | bytes 512
